TPU v7x, 32 devices: a whole 2x2x4 slice. The times are simulated.
32 devices in a mesh: map: 8 (over z, y), rep: 4 (over x, core).
Axes of the slice: x: 2, y: 2, z: 4, core: 2. Of those that a mesh axis runs over, the one named last changes fastest.
Arguments:
- field_bricks: bfloat16 [16384, 512], P('map'), may hold values from -6 to 6
- owners: int32 [2048, 64], P('map', 'rep'), may hold values from 0 to 7, as said below
- bricks: int32 [2048, 64], P('map', 'rep'), may hold values from 0 to 2047
- corners: int32 [2048, 64], P('map', 'rep'), may hold values from 0 to 342
- fraction: float32 [3, 2048, 64], P(None, 'map', 'rep'), may hold values from 0 to 1
Outputs:
- trajectory_cost: float32 [2048], P('map')
- waypoint_grad: float32 [3, 2048, 64], P(None, 'map', 'rep')
Inputs may be any that keep to these rules, and one draw needn't show every extreme that they name: `owners`: among one device's 4096 waypoints at most 2048 have the same owner, and in every draw some owner has exactly 2048 of them.
All inputs are finite; a program needn't handle non-finite values.
Results may differ from a plain program's by a relative error of at most 0.0003.
Values sent between devices are 32-bit elements; how exact they have to be, the bound alone decides.
A program may use at most 64 MiB of HBM per device.

v0:
```python
import functools

import jax
import jax.numpy as jnp
from jax import lax
from jax.experimental import pallas as pl
from jax.experimental.pallas import tpu as pltpu
from jax.sharding import PartitionSpec as P

margin = 0.5
LANES = 128
VMEM = pltpu.VMEM
SMEM = pltpu.SMEM


MESH = pl.DeviceIdType.MESH


def lanes_of(x):
    return jnp.concatenate(
        [x[:, h * LANES : (h + 1) * LANES] for h in range(x.shape[1] // LANES)], axis=0
    )


def iota(shape, axis):
    return lax.broadcasted_iota(jnp.int32, shape, axis)


def stay(x):
    return pltpu.with_memory_space_constraint(x, pltpu.HBM)


def each(count, body, unrolled):
    if count <= unrolled:
        for i in range(count):
            body(i)
    else:
        lax.fori_loop(0, count, lambda i, z: (body(i), z)[1], 0)


def dispatch_kernel(
    devices, tiles, owners_hbm, bricks_hbm, corners_hbm, frac_hbm,
    out_ref, own_ref, rank_ref, meta_ref,
    data_ref, pos_ref, meta_s, sem, owners_ref, bricks_ref, corners_ref, frac_ref, load_sem,
):
    loads = [
        pltpu.make_async_copy(source, target, load_sem.at[i])
        for i, (source, target) in enumerate(
            [(owners_hbm, owners_ref), (bricks_hbm, bricks_ref),
             (corners_hbm, corners_ref), (frac_hbm, frac_ref)]
        )
    ]
    for load in loads:
        load.start()
    out_ref[...] = jnp.zeros_like(out_ref)
    for load in loads:
        load.wait()
    own = lanes_of(owners_ref[...])
    chunks = own.shape[0]
    bricks = bricks_ref[...]
    corners = corners_ref[...]
    cx = (corners * 1338) >> 16
    cxy = (corners * 9363) >> 16
    code = bricks * 512 + cx * 64 + (cxy - cx * 7) * 8 + (corners - cxy * 7)
    code = lanes_of(code.astype(jnp.float32))
    for k in range(2):
        data_ref[:, 4 * k, :] = code
    for f in range(3):
        part = lanes_of(frac_ref[f])
        for k in range(2):
            data_ref[:, 4 * k + 1 + f, :] = part
    own_ref[...] = own

    upper = (iota((LANES, LANES), 0) <= iota((LANES, LANES), 1)).astype(jnp.float32).astype(jnp.bfloat16)
    ones = jnp.ones((LANES, LANES), jnp.bfloat16)
    before = (iota((chunks, chunks), 0) > iota((chunks, chunks), 1)).astype(jnp.float32).astype(jnp.bfloat16)
    lane = iota((chunks, LANES), 1)
    rank = jnp.zeros((chunks, LANES), jnp.float32)
    pos = jnp.zeros((chunks, LANES), jnp.float32)
    start = jnp.zeros((chunks, LANES), jnp.float32)
    meta = jnp.zeros((chunks, LANES), jnp.int32)
    for o in range(devices):
        member = own == o
        m16 = member.astype(jnp.float32).astype(jnp.bfloat16)
        incl = jnp.dot(m16, upper, preferred_element_type=jnp.float32) - 1.0
        total = jnp.dot(m16, ones, preferred_element_type=jnp.float32)
        off = jnp.dot(before, total.astype(jnp.bfloat16), preferred_element_type=jnp.float32)
        rank = jnp.where(member, incl + off, rank)
        pos = jnp.where(member, incl + start, pos)
        meta = jnp.where(lane == o, off.astype(jnp.int32), meta)
        turn = (off - start).astype(jnp.int32) & (LANES - 1)
        meta = jnp.where(lane == devices + o, turn, meta)
        start = start + total
        last = (off + total)[chunks - 1 : chunks, :]
        out_ref[o, 4 * tiles : 4 * tiles + 8, :] = jnp.broadcast_to(last, (8, LANES))
    rank_ref[...] = rank.astype(jnp.int32)
    pos_ref[...] = pos.astype(jnp.int32)
    meta_ref[...] = meta
    copy = pltpu.make_async_copy(meta_ref, meta_s, sem)
    copy.start()

    def sort_chunk(c):
        hot = (iota((LANES, LANES), 0) == pos_ref[pl.ds(c, 1), :]).astype(jnp.float32).astype(jnp.bfloat16)
        items = iota((8, LANES), 1).astype(jnp.float32).astype(jnp.bfloat16)
        inverse = lax.dot_general(
            items, hot, (((1,), (1,)), ((), ())), preferred_element_type=jnp.float32
        ).astype(jnp.int32)
        data_ref[c] = jnp.take_along_axis(data_ref[c], inverse, axis=1, mode="promise_in_bounds")

    for c in range(chunks):
        sort_chunk(c)
    copy.wait()
    sub8 = iota((8, LANES), 0)
    lane8 = iota((8, LANES), 1)

    def place_chunk(c, carry):
        row = data_ref[c]

        def place(o):
            off = meta_s[c, o]
            where_to = pl.ds(4 * (off >> 7), 8)
            turned = pltpu.roll(row, meta_s[c, devices + o], 1)
            keep = (sub8 < 4) & (lane8 < (off & (LANES - 1)))
            out_ref[o, where_to, :] = jnp.where(keep, out_ref[o, where_to, :], turned)

        each(devices, place, 8)
        return carry

    counts = [out_ref[o, 4 * tiles : 4 * tiles + 8, :] for o in range(devices)] if devices <= 8 else None
    if counts is None:
        last_off = meta_ref
    lax.fori_loop(0, chunks, place_chunk, 0)
    for o in range(devices):
        if counts is not None:
            out_ref[o, 4 * tiles : 4 * tiles + 8, :] = counts[o]
        else:
            n = meta_s[chunks - 1, o] + jnp.sum((own_ref[chunks - 1 : chunks, :] == o).astype(jnp.int32))
            out_ref[o, 4 * tiles : 4 * tiles + 8, :] = jnp.full((8, LANES), n, jnp.int32).astype(jnp.float32)


def lookup_kernel(
    devices, tiles, table, in_ref, out_ref, index_v, index_s, rows_ref, sem
):
    span = tiles + 1
    for s in range(devices):
        codes = in_ref[s, pl.ds(0, span, stride=4), :].astype(jnp.int32)
        is_count = iota((span, LANES), 0) == tiles
        index_v[pl.ds(s * span, span), :] = jnp.where(is_count, codes, codes >> 6)
    copy = pltpu.make_async_copy(index_v, index_s, sem)
    copy.start()

    copy.wait()
    sub8 = iota((8, LANES), 0)

    def source(s):
        count = index_s[s * span + tiles, 0]

        def tile(t, carry):
            line = s * span + t
            for p in range(LANES):
                rows_ref[p : p + 1, :] = table[pl.ds(index_s[line, p], 1), :]
            cells = rows_ref[...].T
            query = in_ref[s, pl.ds(4 * t, 4), :]
            code = query[0:1].astype(jnp.int32)
            cy = jnp.broadcast_to((code >> 3) & 7, (8, LANES))
            cz = jnp.broadcast_to(code & 7, (8, LANES))
            fx = jnp.broadcast_to(query[1:2], (8, LANES))
            fy = jnp.broadcast_to(query[2:3], (8, LANES))
            fz = jnp.broadcast_to(query[3:4], (8, LANES))
            zero = jnp.zeros((8, LANES), jnp.float32)
            inter = [zero, zero]
            slope = [zero, zero]
            for y in range(8):
                low, high = cy == y, cy == y - 1
                weight = jnp.where(low, 1.0 - fy, jnp.where(high, fy, 0.0))
                sign = jnp.where(low, -1.0, jnp.where(high, 1.0, 0.0))
                for a in range(2):
                    v = cells[64 * a + 8 * y : 64 * a + 8 * y + 8, :]
                    inter[a] = inter[a] + weight * v
                    slope[a] = slope[a] + sign * v
            low, high = cz == sub8, cz == sub8 - 1
            weight = jnp.where(low, 1.0 - fz, jnp.where(high, fz, 0.0))
            sign = jnp.where(low, -1.0, jnp.where(high, 1.0, 0.0))
            mixed = (1.0 - fx) * inter[0] + fx * inter[1]
            parts = [
                weight * mixed,
                weight * (inter[1] - inter[0]),
                weight * ((1.0 - fx) * slope[0] + fx * slope[1]),
                sign * mixed,
            ]
            out_ref[s, pl.ds(4 * t, 4), :] = jnp.concatenate(
                [jnp.sum(q, axis=0, keepdims=True) for q in parts], axis=0
            )
            return carry

        lax.fori_loop(0, (count + LANES - 1) >> 7, tile, 0)

    lax.fori_loop(0, devices, lambda s, z: (source(s), z)[1], 0)


def greet(peers):
    barrier = pltpu.get_barrier_semaphore()
    for peer in peers:
        pl.semaphore_signal(barrier, inc=1, device_id=peer, device_id_type=MESH)
    pl.semaphore_wait(barrier, len(peers))


def peer_along(axis, size, step):
    return {axis: lax.rem(lax.axis_index(axis) + step, size)}


def starts(devices, lines, src_ref, dst_of, send_sem, recv_sem):
    me = lax.axis_index("map")
    copies = []
    for k in range(1, devices):
        to = lax.rem(me + k, devices)
        copy = pltpu.make_async_remote_copy(
            src_ref=src_ref.at[to, pl.ds(0, lines)],
            dst_ref=dst_of(k),
            send_sem=send_sem.at[k],
            recv_sem=recv_sem.at[k],
            device_id={"map": to},
            device_id_type=MESH,
        )
        copy.start()
        copies.append(copy)
    own = pltpu.make_async_copy(
        src_ref.at[me, pl.ds(0, lines)], dst_of(0), recv_sem.at[0]
    )
    own.start()
    return own, copies


def exchange_kernel(devices, lines, in_ref, field_hbm, out_ref, table, send_sem, recv_sem, field_ref, field_sem):
    load = pltpu.make_async_copy(field_hbm, field_ref, field_sem)
    load.start()
    greet([peer_along("map", devices, k) for k in range(1, devices)])
    me = lax.axis_index("map")
    own, copies = starts(
        devices, lines, in_ref, lambda k: out_ref.at[me, pl.ds(0, lines)], send_sem, recv_sem
    )
    def build(g, carry):
        block = field_ref[pl.ds(pl.multiple_of(g * 16, 16), 16), :].astype(jnp.float32)
        for x in range(7):
            table[pl.ds(g * 128 + x, 16, stride=8), :] = block[:, 64 * x : 64 * x + 128]
        return carry

    load.wait()
    lax.fori_loop(0, field_ref.shape[0] // 16, build, 0)
    own.wait()
    for copy in copies:
        copy.wait()


def combine_kernel(
    devices, reps, lines, in_ref, own_ref, rank_ref, meta_s, cost_ref, grad_ref,
    held, costs, send_sem, recv_sem, cost_send, cost_recv, *landed,
):
    greet(
        [peer_along("map", devices, k) for k in range(1, devices)]
        + [peer_along("rep", reps, k) for k in range(1, reps)]
    )
    own_copy, copies = starts(
        devices, lines, in_ref, lambda k: landed[k].at[pl.ds(0, lines)], send_sem, recv_sem
    )
    me = lax.axis_index("map")
    chunks = own_ref.shape[0]
    sub8 = iota((8, LANES), 0)
    half = (sub8 >= 4).astype(jnp.int32)
    for k in range(devices):
        if k == 0:
            own_copy.wait()
            source = me
        else:
            copies[k - 1].wait_recv()
            source = lax.rem(me + devices - k, devices)

        def chunk(c, carry):
            owner = jnp.broadcast_to(own_ref[pl.ds(c, 1), :], (8, LANES))
            rank = jnp.broadcast_to(rank_ref[pl.ds(c, 1), :], (8, LANES))
            which = (rank >> 7) - half
            w = meta_s[c, source] >> 7
            picked = jnp.take_along_axis(
                landed[k][pl.ds(4 * w, 8), :], rank & (LANES - 1), axis=1,
                mode="promise_in_bounds",
            )
            before = held[c] if k else jnp.zeros((8, LANES), jnp.float32)
            held[c] = jnp.where((owner == source) & (which == w), picked, before)
            return carry

        lax.fori_loop(0, chunks, chunk, 0, unroll=8)
    dist = held[:, 0, :] + held[:, 4, :]
    hinge = jnp.maximum(margin - dist, 0.0)
    halves = grad_ref.shape[2] // LANES
    quarter = chunks // halves
    rep = lax.axis_index("rep")
    for h in range(halves):
        here = hinge[h * quarter : (h + 1) * quarter]
        costs[0, :, h * LANES : (h + 1) * LANES] = jnp.sum(here * here, axis=0, keepdims=True)
    for n in range(3):
        grad = -2.0 * hinge * (held[:, 1 + n, :] + held[:, 5 + n, :])
        for h in range(halves):
            grad_ref[n, :, h * LANES : (h + 1) * LANES] = grad[h * quarter : (h + 1) * quarter]
    sums = []
    for k in range(1, reps):
        copy = pltpu.make_async_remote_copy(
            src_ref=costs.at[0],
            dst_ref=costs.at[k],
            send_sem=cost_send.at[k],
            recv_sem=cost_recv.at[k],
            device_id=peer_along("rep", reps, k),
            device_id_type=MESH,
        )
        copy.start()
        sums.append(copy)
    for copy in copies:
        copy.wait_send()
    total = costs[0]
    for k, copy in enumerate(sums):
        copy.wait()
        total = total + costs[k + 1]
    cost_ref[...] = total


def per_device(field_bricks, owners, bricks, corners, fraction):
    devices = lax.axis_size("map")
    trajectories_here, quarter = owners.shape
    row_count = trajectories_here * quarter
    capacity = 4 * row_count // devices
    tiles = -(-capacity // LANES)
    chunks = row_count // LANES
    lines = -(-(4 * tiles + 8) // 8) * 8
    buffer = jax.ShapeDtypeStruct((devices, lines, LANES), jnp.float32)
    flat = jax.ShapeDtypeStruct((chunks, LANES), jnp.int32)
    vm = pl.BlockSpec(memory_space=VMEM)
    sm = pl.BlockSpec(memory_space=SMEM)
    hbm = pl.BlockSpec(memory_space=pltpu.HBM)
    whole = VMEM((quarter, trajectories_here), jnp.int32)
    outgoing, own, rank, meta = pl.pallas_call(
        functools.partial(dispatch_kernel, devices, tiles),
        out_shape=(buffer, flat, flat, flat),
        in_specs=[hbm] * 4,
        out_specs=(vm,) * 4,
        scratch_shapes=[
            VMEM((chunks, 8, LANES), jnp.float32),
            VMEM((chunks, LANES), jnp.int32),
            SMEM((chunks, LANES), jnp.int32),
            pltpu.SemaphoreType.DMA(()),
            whole, whole, whole,
            VMEM((3, quarter, trajectories_here), jnp.float32),
            pltpu.SemaphoreType.DMA((4,)),
        ],
        compiler_params=pltpu.CompilerParams(vmem_limit_bytes=16 << 20),
        name="dispatch",
    )(*(stay(x) for x in (owners.T, bricks.T, corners.T, fraction.transpose(0, 2, 1))))
    span = tiles + 1
    sems = pltpu.SemaphoreType.DMA((devices,))
    table = VMEM((field_bricks.shape[0] * 8, LANES), jnp.float32)
    incoming, table = pl.pallas_call(
        functools.partial(exchange_kernel, devices, 4 * span),
        out_shape=(buffer, table),
        in_specs=[vm, hbm],
        out_specs=(vm, vm),
        scratch_shapes=[
            sems, sems, VMEM(field_bricks.shape, field_bricks.dtype), pltpu.SemaphoreType.DMA(()),
        ],
        compiler_params=pltpu.CompilerParams(collective_id=0, has_side_effects=True, vmem_limit_bytes=16 << 20),
        name="send_queries",
    )(outgoing, stay(field_bricks))
    located = pl.pallas_call(
        functools.partial(lookup_kernel, devices, tiles),
        out_shape=buffer,
        in_specs=[vm] * 2,
        out_specs=vm,
        scratch_shapes=[
            VMEM((devices * span, LANES), jnp.int32),
            SMEM((devices * span, LANES), jnp.int32),
            VMEM((LANES, LANES), jnp.float32),
            pltpu.SemaphoreType.DMA(()),
        ],
        compiler_params=pltpu.CompilerParams(vmem_limit_bytes=16 << 20),
        name="lookup",
    )(table, incoming)
    reps = lax.axis_size("rep")
    rep_sems = pltpu.SemaphoreType.DMA((reps,))
    cost, waypoint_grad = pl.pallas_call(
        functools.partial(combine_kernel, devices, reps, 4 * tiles),
        out_shape=(
            jax.ShapeDtypeStruct((1, trajectories_here), jnp.float32),
            jax.ShapeDtypeStruct((3, quarter, trajectories_here), jnp.float32),
        ),
        in_specs=[vm, vm, vm, sm],
        out_specs=(vm, vm),
        scratch_shapes=[
            VMEM((chunks, 8, LANES), jnp.float32),
            VMEM((reps, 1, trajectories_here), jnp.float32),
            sems, sems, rep_sems, rep_sems,
        ]
        + [VMEM((lines, LANES), jnp.float32)] * devices,
        compiler_params=pltpu.CompilerParams(collective_id=1, has_side_effects=True, vmem_limit_bytes=16 << 20),
        name="combine",
    )(located, own, rank, meta)
    return cost.reshape(trajectories_here), waypoint_grad.transpose(0, 2, 1)


def solution(mesh):
    placed = (
        P("map", None),
        P("map", "rep"),
        P("map", "rep"),
        P("map", "rep"),
        P(None, "map", "rep"),
    )
    return jax.shard_map(
        per_device,
        mesh=mesh,
        in_specs=placed,
        out_specs=(P("map"), P(None, "map", "rep")),
        check_vma=False,
    )
```

profile of v0, /device:TPU:0, one launch (start us, length us, event | category | flops | bytes accessed | tf_op | source)
XLA Modules:
  0.0 52.1 jit_solution(8773730951250649032)
XLA Ops:
  0.6 5.8 %dispatch.1 = (f32[8,72,128]{2,1,0:T(8,128)S(1)}, s32[32,128]{1,0:T(8,128)S(1)}, s32[32,128]{1,0:T(8,128)S(1)}, s32[32,128]{1,0:T(8,128)S(1)}) custom-call(s32[16,256]{1,0:T(8,128)} %bitcast.9, s32[16,256]{1,0:T(8,128)} %bitcast.10, s32[16,256]{1,0:T(8,128)} %bitcast.11, f32[3,16,256]{2,1,0:T(8,128)} %bitcast.8), custom_call_target="tpu_custom_call" | custom-call | tf_op jit(solution)/shard_map/dispatch/pallas_call | solution.py:339
  6.4 16.0 %send_queries.1 = (f32[8,72,128]{2,1,0:T(8,128)S(1)}, f32[16384,128]{1,0:T(8,128)S(1)}) custom-call(f32[8,72,128]{2,1,0:T(8,128)S(1)} %get-tuple-element.10.in_ref, bf16[2048,512]{1,0:T(8,128)(2,1)} %field_hbm.1), custom_call_target="tpu_custom_call" | custom-call | tf_op jit(solution)/shard_map/send_queries/pallas_call | solution.py:359
  22.5 6.4 %lookup.1.in_ref = f32[8,72,128]{2,1,0:T(8,128)S(1)} custom-call(f32[16384,128]{1,0:T(8,128)S(1)} %get-tuple-element.11.table, f32[8,72,128]{2,1,0:T(8,128)S(1)} %get-tuple-element.12.in_ref), custom_call_target="tpu_custom_call" | custom-call | tf_op jit(solution)/shard_map/lookup/pallas_call | solution.py:370
  28.9 22.0 %combine.1 = (f32[1,256]{1,0:T(1,128)S(1)}, f32[3,16,256]{2,1,0:T(8,128)S(1)}) custom-call(f32[8,72,128]{2,1,0:T(8,128)S(1)} %lookup.1.in_ref, s32[32,128]{1,0:T(8,128)S(1)} %get-tuple-element.13.own_ref, s32[32,128]{1,0:T(8,128)S(1)} %get-tuple-element.14.rank_ref, s32[32,128]{1,0:T(8,128)S(1)} %get-tuple-element.15.meta_s), custom_call_target="tpu_custom_call" | custom-call | tf_op jit(solution)/shard_map/combine/pallas_call | solution.py:386
  50.9 0.6 %copy.9 = f32[256]{0:T(256)} copy(f32[256]{0:T(256)S(1)} %bitcast.7) | data formatting | bytes 2048
  51.4 0.6 %copy.10 = f32[3,256,16]{1,2,0:T(8,128)} copy(f32[3,256,16]{1,2,0:T(8,128)S(1)} %bitcast.6) | data formatting | bytes 98304
where the time goes:
time: 51.5 us; the launch traced here: 52.1 us
  Pallas kernels  50.2 us (97%)
  local copies, waits for them, and re-layouts  1.18 us (2%)
  between operations  0.66 us (1%)
    pallas_call x1, Pallas kernels, per_device(): pl.pallas_call(functools.partial(combine_kernel, devices, reps, 4 * tiles...  22 us
    pallas_call x1, Pallas kernels, per_device(): pl.pallas_call(functools.partial(exchange_kernel, devices, 4 * span), out...  16 us
    pallas_call x1, Pallas kernels, per_device(): pl.pallas_call(functools.partial(lookup_kernel, devices, tiles), out_shap...  6.42 us
    pallas_call x1, Pallas kernels, per_device(): pl.pallas_call(functools.partial(dispatch_kernel, devices, tiles), out_sh...  5.79 us
    unnamed x2, local copies, waits for them, and re-layouts  1.18 us

commit v1 on v0

--- a/solution.py
+++ b/solution.py
@@ -129,7 +129,7 @@
     counts = [out_ref[o, 4 * tiles : 4 * tiles + 8, :] for o in range(devices)] if devices <= 8 else None
     if counts is None:
         last_off = meta_ref
-    lax.fori_loop(0, chunks, place_chunk, 0)
+    lax.fori_loop(0, chunks, place_chunk, 0, unroll=4 if devices <= 8 else 1)
     for o in range(devices):
         if counts is not None:
             out_ref[o, 4 * tiles : 4 * tiles + 8, :] = counts[o]
@@ -139,63 +139,87 @@
 
 
 def lookup_kernel(
-    devices, tiles, table, in_ref, out_ref, index_v, index_s, rows_ref, sem
+    devices, tiles, table, in_ref, out_ref, index_v, index_s, rows_a, rows_b, sem
 ):
     span = tiles + 1
+    bricks = table.shape[0] // 7
     for s in range(devices):
         codes = in_ref[s, pl.ds(0, span, stride=4), :].astype(jnp.int32)
         is_count = iota((span, LANES), 0) == tiles
-        index_v[pl.ds(s * span, span), :] = jnp.where(is_count, codes, codes >> 6)
+        row = ((codes >> 6) & 7) * bricks + (codes >> 9)
+        used = jnp.maximum((codes + LANES - 1) >> 7, 1)
+        index_v[pl.ds(s * span, span), :] = jnp.where(is_count, used, row)
     copy = pltpu.make_async_copy(index_v, index_s, sem)
     copy.start()
-
     copy.wait()
     sub8 = iota((8, LANES), 0)
 
-    def source(s):
-        count = index_s[s * span + tiles, 0]
-
-        def tile(t, carry):
-            line = s * span + t
-            for p in range(LANES):
-                rows_ref[p : p + 1, :] = table[pl.ds(index_s[line, p], 1), :]
-            cells = rows_ref[...].T
-            query = in_ref[s, pl.ds(4 * t, 4), :]
-            code = query[0:1].astype(jnp.int32)
-            cy = jnp.broadcast_to((code >> 3) & 7, (8, LANES))
-            cz = jnp.broadcast_to(code & 7, (8, LANES))
-            fx = jnp.broadcast_to(query[1:2], (8, LANES))
-            fy = jnp.broadcast_to(query[2:3], (8, LANES))
-            fz = jnp.broadcast_to(query[3:4], (8, LANES))
-            zero = jnp.zeros((8, LANES), jnp.float32)
-            inter = [zero, zero]
-            slope = [zero, zero]
-            for y in range(8):
-                low, high = cy == y, cy == y - 1
-                weight = jnp.where(low, 1.0 - fy, jnp.where(high, fy, 0.0))
-                sign = jnp.where(low, -1.0, jnp.where(high, 1.0, 0.0))
-                for a in range(2):
-                    v = cells[64 * a + 8 * y : 64 * a + 8 * y + 8, :]
-                    inter[a] = inter[a] + weight * v
-                    slope[a] = slope[a] + sign * v
-            low, high = cz == sub8, cz == sub8 - 1
-            weight = jnp.where(low, 1.0 - fz, jnp.where(high, fz, 0.0))
+    def used_of(s):
+        return index_s[s * span + tiles, 0]
+
+    def following(s, t):
+        more = t + 1 < used_of(s)
+        last = s + 1 >= devices
+        t_next = jnp.where(more, t + 1, jnp.where(last, t, 0))
+        s_next = jnp.where(more | last, s, s + 1)
+        return s_next, t_next
+
+    def gather(s, t, rows):
+        line = index_s.at[s * span + t]
+        for p in range(LANES):
+            rows[p : p + 1, :] = table[pl.ds(line[p], 1), :]
+
+    def weigh(s, t, rows):
+        cells = rows[...].T
+        query = in_ref[s, pl.ds(4 * t, 4), :]
+        code = query[0:1].astype(jnp.int32)
+        cy = jnp.broadcast_to((code >> 3) & 7, (8, LANES))
+        cz = jnp.broadcast_to(code & 7, (8, LANES))
+        fx = jnp.broadcast_to(query[1:2], (8, LANES))
+        fy = jnp.broadcast_to(query[2:3], (8, LANES))
+        fz = jnp.broadcast_to(query[3:4], (8, LANES))
+        zero = jnp.zeros((8, LANES), jnp.float32)
+        inter = [zero, zero]
+        slope = [zero, zero]
+        for y in range(8):
+            low, high = cy == y, cy == y - 1
+            weight = jnp.where(low, 1.0 - fy, jnp.where(high, fy, 0.0))
             sign = jnp.where(low, -1.0, jnp.where(high, 1.0, 0.0))
-            mixed = (1.0 - fx) * inter[0] + fx * inter[1]
-            parts = [
-                weight * mixed,
-                weight * (inter[1] - inter[0]),
-                weight * ((1.0 - fx) * slope[0] + fx * slope[1]),
-                sign * mixed,
-            ]
-            out_ref[s, pl.ds(4 * t, 4), :] = jnp.concatenate(
-                [jnp.sum(q, axis=0, keepdims=True) for q in parts], axis=0
-            )
-            return carry
-
-        lax.fori_loop(0, (count + LANES - 1) >> 7, tile, 0)
-
-    lax.fori_loop(0, devices, lambda s, z: (source(s), z)[1], 0)
+            for a in range(2):
+                v = cells[64 * a + 8 * y : 64 * a + 8 * y + 8, :]
+                inter[a] = inter[a] + weight * v
+                slope[a] = slope[a] + sign * v
+        low, high = cz == sub8, cz == sub8 - 1
+        weight = jnp.where(low, 1.0 - fz, jnp.where(high, fz, 0.0))
+        sign = jnp.where(low, -1.0, jnp.where(high, 1.0, 0.0))
+        mixed = (1.0 - fx) * inter[0] + fx * inter[1]
+        parts = [
+            weight * mixed,
+            weight * (inter[1] - inter[0]),
+            weight * ((1.0 - fx) * slope[0] + fx * slope[1]),
+            sign * mixed,
+        ]
+        out_ref[s, pl.ds(4 * t, 4), :] = jnp.concatenate(
+            [jnp.sum(q, axis=0, keepdims=True) for q in parts], axis=0
+        )
+
+    total = used_of(0)
+    for s in range(1, devices):
+        total = total + used_of(s)
+
+    def pair(i, now):
+        s0, t0 = now
+        s1, t1 = following(s0, t0)
+        s2, t2 = following(s1, t1)
+        gather(s1, t1, rows_b)
+        weigh(s0, t0, rows_a)
+        gather(s2, t2, rows_a)
+        weigh(s1, t1, rows_b)
+        return s2, t2
+
+    first = (jnp.int32(0), jnp.int32(0))
+    gather(*first, rows_a)
+    lax.fori_loop(0, (total + 1) >> 1, pair, first)
 
 
 def greet(peers):
@@ -239,14 +263,16 @@
     own, copies = starts(
         devices, lines, in_ref, lambda k: out_ref.at[me, pl.ds(0, lines)], send_sem, recv_sem
     )
+    bricks = field_ref.shape[0]
+
     def build(g, carry):
         block = field_ref[pl.ds(pl.multiple_of(g * 16, 16), 16), :].astype(jnp.float32)
         for x in range(7):
-            table[pl.ds(g * 128 + x, 16, stride=8), :] = block[:, 64 * x : 64 * x + 128]
+            table[pl.ds(pl.multiple_of(x * bricks + g * 16, 16), 16), :] = block[:, 64 * x : 64 * x + 128]
         return carry
 
     load.wait()
-    lax.fori_loop(0, field_ref.shape[0] // 16, build, 0)
+    lax.fori_loop(0, bricks // 16, build, 0, unroll=8)
     own.wait()
     for copy in copies:
         copy.wait()
@@ -267,40 +293,34 @@
     chunks = own_ref.shape[0]
     sub8 = iota((8, LANES), 0)
     half = (sub8 >= 4).astype(jnp.int32)
-    for k in range(devices):
-        if k == 0:
-            own_copy.wait()
-            source = me
-        else:
-            copies[k - 1].wait_recv()
+    own_copy.wait()
+    for copy in copies:
+        copy.wait_recv()
+
+    def chunk(c, carry):
+        owner = jnp.broadcast_to(own_ref[pl.ds(c, 1), :], (8, LANES))
+        rank = jnp.broadcast_to(rank_ref[pl.ds(c, 1), :], (8, LANES))
+        lane = rank & (LANES - 1)
+        which = (rank >> 7) - half
+        value = jnp.zeros((8, LANES), jnp.float32)
+        for k in range(devices):
             source = lax.rem(me + devices - k, devices)
-
-        def chunk(c, carry):
-            owner = jnp.broadcast_to(own_ref[pl.ds(c, 1), :], (8, LANES))
-            rank = jnp.broadcast_to(rank_ref[pl.ds(c, 1), :], (8, LANES))
-            which = (rank >> 7) - half
             w = meta_s[c, source] >> 7
             picked = jnp.take_along_axis(
-                landed[k][pl.ds(4 * w, 8), :], rank & (LANES - 1), axis=1,
-                mode="promise_in_bounds",
+                landed[k][pl.ds(4 * w, 8), :], lane, axis=1, mode="promise_in_bounds"
             )
-            before = held[c] if k else jnp.zeros((8, LANES), jnp.float32)
-            held[c] = jnp.where((owner == source) & (which == w), picked, before)
-            return carry
-
-        lax.fori_loop(0, chunks, chunk, 0, unroll=8)
+            value = jnp.where((owner == source) & (which == w), picked, value)
+        held[c] = value
+        return carry
+
+    lax.fori_loop(0, chunks, chunk, 0, unroll=4 if devices <= 8 else 1)
     dist = held[:, 0, :] + held[:, 4, :]
     hinge = jnp.maximum(margin - dist, 0.0)
     halves = grad_ref.shape[2] // LANES
     quarter = chunks // halves
-    rep = lax.axis_index("rep")
     for h in range(halves):
         here = hinge[h * quarter : (h + 1) * quarter]
         costs[0, :, h * LANES : (h + 1) * LANES] = jnp.sum(here * here, axis=0, keepdims=True)
-    for n in range(3):
-        grad = -2.0 * hinge * (held[:, 1 + n, :] + held[:, 5 + n, :])
-        for h in range(halves):
-            grad_ref[n, :, h * LANES : (h + 1) * LANES] = grad[h * quarter : (h + 1) * quarter]
     sums = []
     for k in range(1, reps):
         copy = pltpu.make_async_remote_copy(
@@ -313,6 +333,10 @@
         )
         copy.start()
         sums.append(copy)
+    for n in range(3):
+        grad = -2.0 * hinge * (held[:, 1 + n, :] + held[:, 5 + n, :])
+        for h in range(halves):
+            grad_ref[n, :, h * LANES : (h + 1) * LANES] = grad[h * quarter : (h + 1) * quarter]
     for copy in copies:
         copy.wait_send()
     total = costs[0]
@@ -320,6 +344,17 @@
         copy.wait()
         total = total + costs[k + 1]
     cost_ref[...] = total
+
+
+def finish_kernel(cost_in, grad_in, cost_out, grad_out, sem):
+    copies = [
+        pltpu.make_async_copy(grad_in, grad_out, sem.at[0]),
+        pltpu.make_async_copy(cost_in, cost_out, sem.at[1]),
+    ]
+    for copy in copies:
+        copy.start()
+    for copy in copies:
+        copy.wait()
 
 
 def per_device(field_bricks, owners, bricks, corners, fraction):
@@ -355,7 +390,7 @@
     )(*(stay(x) for x in (owners.T, bricks.T, corners.T, fraction.transpose(0, 2, 1))))
     span = tiles + 1
     sems = pltpu.SemaphoreType.DMA((devices,))
-    table = VMEM((field_bricks.shape[0] * 8, LANES), jnp.float32)
+    table = VMEM((field_bricks.shape[0] * 7, LANES), jnp.float32)
     incoming, table = pl.pallas_call(
         functools.partial(exchange_kernel, devices, 4 * span),
         out_shape=(buffer, table),
@@ -375,6 +410,7 @@
         scratch_shapes=[
             VMEM((devices * span, LANES), jnp.int32),
             SMEM((devices * span, LANES), jnp.int32),
+            VMEM((LANES, LANES), jnp.float32),
             VMEM((LANES, LANES), jnp.float32),
             pltpu.SemaphoreType.DMA(()),
         ],
@@ -400,6 +436,18 @@
         compiler_params=pltpu.CompilerParams(collective_id=1, has_side_effects=True, vmem_limit_bytes=16 << 20),
         name="combine",
     )(located, own, rank, meta)
+    cost, waypoint_grad = pl.pallas_call(
+        finish_kernel,
+        out_shape=(
+            jax.ShapeDtypeStruct(cost.shape, jnp.float32),
+            jax.ShapeDtypeStruct(waypoint_grad.shape, jnp.float32),
+        ),
+        in_specs=[vm] * 2,
+        out_specs=(hbm,) * 2,
+        scratch_shapes=[pltpu.SemaphoreType.DMA((2,))],
+        compiler_params=pltpu.CompilerParams(vmem_limit_bytes=1 << 20),
+        name="finish",
+    )(cost, waypoint_grad)
     return cost.reshape(trajectories_here), waypoint_grad.transpose(0, 2, 1)
 
 

time: 51.5 us -> 42.4 us (0.82); the launches traced: 52.1 us -> 42.2 us
  Pallas kernels: 50.2 us -> 41.5 us
  local copies, waits for them, and re-layouts: 1.18 us -> 0 us
    pallas_call x1, Pallas kernels: 16 us -> 11 us  [per_device(): pl.pallas_call(functools.partial(exchange_kernel, devices, 4 * span), out...]
    pallas_call x1, Pallas kernels: 6.42 us -> 4.15 us  [per_device(): pl.pallas_call(functools.partial(lookup_kernel, devices, tiles), out_shap...]
    pallas_call x1, Pallas kernels: 5.79 us -> 4.47 us  [per_device(): pl.pallas_call(functools.partial(dispatch_kernel, devices, tiles), out_sh...]
    unnamed x2 -> x0, local copies, waits for them, and re-layouts: 1.18 us -> none
    pallas_call x1, Pallas kernels: 22 us -> 21.2 us  [per_device(): pl.pallas_call(functools.partial(combine_kernel, devices, reps, 4 * tiles...]
    pallas_call x0 -> x1, Pallas kernels: none -> 0.64 us  [per_device(): pl.pallas_call(finish_kernel, out_shape=(jax.ShapeDtypeStruct(cost.shape,...]
where the time goes in v1:
time: 42.4 us; the launch traced here: 42.2 us
  Pallas kernels  41.5 us (98%)
  between operations  0.66 us (2%)
    pallas_call x1, Pallas kernels, per_device(): pl.pallas_call(functools.partial(combine_kernel, devices, reps, 4 * tiles...  21.2 us
    pallas_call x1, Pallas kernels, per_device(): pl.pallas_call(functools.partial(exchange_kernel, devices, 4 * span), out...  11 us
    pallas_call x1, Pallas kernels, per_device(): pl.pallas_call(functools.partial(dispatch_kernel, devices, tiles), out_sh...  4.47 us
    pallas_call x1, Pallas kernels, per_device(): pl.pallas_call(functools.partial(lookup_kernel, devices, tiles), out_shap...  4.15 us

profile of v1, /device:TPU:0, one launch (start us, length us, event | category | flops | bytes accessed | tf_op | source)
XLA Modules:
  0.0 42.2 jit_solution(15446354597612252291)
XLA Ops:
  0.6 4.5 %dispatch.1 = (f32[8,72,128]{2,1,0:T(8,128)S(1)}, s32[32,128]{1,0:T(8,128)S(1)}, s32[32,128]{1,0:T(8,128)S(1)}, s32[32,128]{1,0:T(8,128)S(1)}) custom-call(s32[16,256]{1,0:T(8,128)} %bitcast.7, s32[16,256]{1,0:T(8,128)} %bitcast.8, s32[16,256]{1,0:T(8,128)} %bitcast.9, f32[3,16,256]{2,1,0:T(8,128)} %bitcast.6), custom_call_target="tpu_custom_call" | custom-call | tf_op jit(solution)/shard_map/dispatch/pallas_call | solution.py:374
  5.1 11.0 %send_queries.1 = (f32[8,72,128]{2,1,0:T(8,128)S(1)}, f32[14336,128]{1,0:T(8,128)S(1)}) custom-call(f32[8,72,128]{2,1,0:T(8,128)S(1)} %get-tuple-element.12.in_ref, bf16[2048,512]{1,0:T(8,128)(2,1)} %field_hbm.1), custom_call_target="tpu_custom_call" | custom-call | tf_op jit(solution)/shard_map/send_queries/pallas_call | solution.py:394
  16.2 4.1 %lookup.1.in_ref = f32[8,72,128]{2,1,0:T(8,128)S(1)} custom-call(f32[14336,128]{1,0:T(8,128)S(1)} %get-tuple-element.13.table, f32[8,72,128]{2,1,0:T(8,128)S(1)} %get-tuple-element.14.in_ref), custom_call_target="tpu_custom_call" | custom-call | tf_op jit(solution)/shard_map/lookup/pallas_call | solution.py:405
  20.3 21.2 %combine.1 = (f32[1,256]{1,0:T(1,128)S(1)}, f32[3,16,256]{2,1,0:T(8,128)S(1)}) custom-call(f32[8,72,128]{2,1,0:T(8,128)S(1)} %lookup.1.in_ref, s32[32,128]{1,0:T(8,128)S(1)} %get-tuple-element.15.own_ref, s32[32,128]{1,0:T(8,128)S(1)} %get-tuple-element.16.rank_ref, s32[32,128]{1,0:T(8,128)S(1)} %get-tuple-element.17.meta_s), custom_call_target="tpu_custom_call" | custom-call | tf_op jit(solution)/shard_map/combine/pallas_call | solution.py:422
  41.5 0.6 %finish.1 = (f32[1,256]{1,0:T(1,128)}, f32[3,16,256]{2,1,0:T(8,128)}) custom-call(f32[1,256]{1,0:T(1,128)S(1)} %get-tuple-element.18.cost_in, f32[3,16,256]{2,1,0:T(8,128)S(1)} %get-tuple-element.19.grad_in), custom_call_target="tpu_custom_call" | custom-call | tf_op jit(solution)/shard_map/finish/pallas_call | solution.py:439

commit v2 on v1

v2 whole, which is shorter than its diff:
```python
import functools

import jax
import jax.numpy as jnp
from jax import lax
from jax.experimental import pallas as pl
from jax.experimental.pallas import tpu as pltpu
from jax.sharding import PartitionSpec as P

margin = 0.5
LANES = 128
VMEM = pltpu.VMEM
SMEM = pltpu.SMEM


MESH = pl.DeviceIdType.MESH


def lanes_of(x):
    return jnp.concatenate(
        [x[:, h * LANES : (h + 1) * LANES] for h in range(x.shape[1] // LANES)], axis=0
    )


def iota(shape, axis):
    return lax.broadcasted_iota(jnp.int32, shape, axis)


def stay(x):
    return pltpu.with_memory_space_constraint(x, pltpu.HBM)


def each(count, body, unrolled):
    if count <= unrolled:
        for i in range(count):
            body(i)
    else:
        lax.fori_loop(0, count, lambda i, z: (body(i), z)[1], 0)


def dispatch_kernel(
    devices, tiles, owners_hbm, bricks_hbm, corners_hbm, frac_hbm,
    out_ref, own_ref, rank_ref, meta_ref,
    data_ref, pos_ref, meta_s, sem, owners_ref, bricks_ref, corners_ref, frac_ref, load_sem,
):
    loads = [
        pltpu.make_async_copy(source, target, load_sem.at[i])
        for i, (source, target) in enumerate(
            [(owners_hbm, owners_ref), (bricks_hbm, bricks_ref),
             (corners_hbm, corners_ref), (frac_hbm, frac_ref)]
        )
    ]
    for load in loads:
        load.start()
    out_ref[...] = jnp.zeros_like(out_ref)
    for load in loads:
        load.wait()
    own = lanes_of(owners_ref[...])
    chunks = own.shape[0]
    bricks = bricks_ref[...]
    corners = corners_ref[...]
    cx = (corners * 1338) >> 16
    cxy = (corners * 9363) >> 16
    code = bricks * 512 + cx * 64 + (cxy - cx * 7) * 8 + (corners - cxy * 7)
    code = lanes_of(code.astype(jnp.float32))
    for k in range(2):
        data_ref[:, 4 * k, :] = code
    for f in range(3):
        part = lanes_of(frac_ref[f])
        for k in range(2):
            data_ref[:, 4 * k + 1 + f, :] = part
    own_ref[...] = own

    upper = (iota((LANES, LANES), 0) <= iota((LANES, LANES), 1)).astype(jnp.float32).astype(jnp.bfloat16)
    ones = jnp.ones((LANES, LANES), jnp.bfloat16)
    before = (iota((chunks, chunks), 0) > iota((chunks, chunks), 1)).astype(jnp.float32).astype(jnp.bfloat16)
    lane = iota((chunks, LANES), 1)
    rank = jnp.zeros((chunks, LANES), jnp.float32)
    pos = jnp.zeros((chunks, LANES), jnp.float32)
    start = jnp.zeros((chunks, LANES), jnp.float32)
    meta = jnp.zeros((chunks, LANES), jnp.int32)
    for o in range(devices):
        member = own == o
        m16 = member.astype(jnp.float32).astype(jnp.bfloat16)
        incl = jnp.dot(m16, upper, preferred_element_type=jnp.float32) - 1.0
        total = jnp.dot(m16, ones, preferred_element_type=jnp.float32)
        off = jnp.dot(before, total.astype(jnp.bfloat16), preferred_element_type=jnp.float32)
        rank = jnp.where(member, incl + off, rank)
        pos = jnp.where(member, incl + start, pos)
        meta = jnp.where(lane == o, off.astype(jnp.int32), meta)
        turn = (off - start).astype(jnp.int32) & (LANES - 1)
        meta = jnp.where(lane == devices + o, turn, meta)
        start = start + total
    rank_ref[...] = rank.astype(jnp.int32)
    pos_ref[...] = pos.astype(jnp.int32)
    meta_ref[...] = meta
    copy = pltpu.make_async_copy(meta_ref, meta_s, sem)
    copy.start()

    def sort_chunk(c):
        hot = (iota((LANES, LANES), 0) == pos_ref[pl.ds(c, 1), :]).astype(jnp.float32).astype(jnp.bfloat16)
        items = iota((8, LANES), 1).astype(jnp.float32).astype(jnp.bfloat16)
        inverse = lax.dot_general(
            items, hot, (((1,), (1,)), ((), ())), preferred_element_type=jnp.float32
        ).astype(jnp.int32)
        data_ref[c] = jnp.take_along_axis(data_ref[c], inverse, axis=1, mode="promise_in_bounds")

    for c in range(chunks):
        sort_chunk(c)
    copy.wait()
    sub8 = iota((8, LANES), 0)
    lane8 = iota((8, LANES), 1)

    def place_chunk(c, carry):
        row = data_ref[c]

        def place(o):
            off = meta_s[c, o]
            where_to = pl.ds(4 * (off >> 7), 8)
            turned = pltpu.roll(row, meta_s[c, devices + o], 1)
            keep = (sub8 < 4) & (lane8 < (off & (LANES - 1)))
            out_ref[o, where_to, :] = jnp.where(keep, out_ref[o, where_to, :], turned)

        each(devices, place, 8)
        return carry

    lax.fori_loop(0, chunks, place_chunk, 0, unroll=4 if devices <= 8 else 1)


def greet(peers):
    barrier = pltpu.get_barrier_semaphore()
    for peer in peers:
        pl.semaphore_signal(barrier, inc=1, device_id=peer, device_id_type=MESH)
    return lambda: pl.semaphore_wait(barrier, len(peers))


def peer_along(axis, size, step):
    return {axis: lax.rem(lax.axis_index(axis) + step, size)}


def batch_of(tiles):
    return max(n for n in (4, 2, 1) if (tiles // 2) % n == 0)


def fused_kernel(
    devices, reps, tiles, out_in, field_hbm, own_ref, rank_ref, meta_ref, cost_ref, grad_ref,
    meta_s, table, field_ref, incoming, answers, landed, landed_last, index_v, index_s, rows, cells, held, costs,
    field_sem, meta_sem, index_sem, query_send, query_recv, answer_send, answer_recv, cost_send, cost_recv,
):
    lines = 4 * tiles
    pairs = tiles // 2
    total = devices * pairs
    batch = batch_of(tiles)
    batches = pairs // batch
    bricks = field_ref.shape[0]
    me = lax.axis_index("map")
    load = pltpu.make_async_copy(field_hbm, field_ref, field_sem)
    load.start()
    meta_copy = pltpu.make_async_copy(meta_ref, meta_s, meta_sem)
    meta_copy.start()
    wait_peers = greet(
        [peer_along("map", devices, k) for k in range(1, devices)]
        + [peer_along("rep", reps, k) for k in range(1, reps)]
    )

    def ahead(k):
        return lax.rem(me + k, devices)

    def behind(k):
        return lax.rem(me + devices - k, devices)

    def query_copy(k):
        return pltpu.make_async_remote_copy(
            src_ref=out_in.at[ahead(k), pl.ds(0, lines)],
            dst_ref=incoming.at[pl.ds(pl.multiple_of(k * lines, 8), lines)],
            send_sem=query_send.at[k],
            recv_sem=query_recv.at[k],
            device_id={"map": ahead(k)},
            device_id_type=MESH,
        )

    def answer_copy(k, last=False):
        return pltpu.make_async_remote_copy(
            src_ref=answers.at[pl.ds(pl.multiple_of(k * lines, 8), lines)],
            dst_ref=(landed_last if last else landed.at[k]).at[pl.ds(0, lines)],
            send_sem=answer_send.at[k],
            recv_sem=answer_recv.at[k],
            device_id={"map": behind(k)},
            device_id_type=MESH,
        )

    incoming[0:lines] = out_in[me, 0:lines]
    rows[...] = jnp.zeros_like(rows)
    cells[...] = jnp.zeros_like(cells)

    def build(g, carry):
        block = field_ref[pl.ds(pl.multiple_of(g * 16, 16), 16), :].astype(jnp.float32)
        for x in range(7):
            table[pl.ds(pl.multiple_of(x * bricks + g * 16, 16), 16), :] = block[:, 64 * x : 64 * x + 128]
        return carry

    wait_peers()
    each(devices - 1, lambda k: query_copy(k + 1).start(), 8)
    load.wait()
    lax.fori_loop(0, bricks // 16, build, 0, unroll=32)

    def index_copy(slot):
        return pltpu.make_async_copy(index_v.at[slot], index_s.at[slot], index_sem.at[slot])

    def start_index(j, slot):
        first = pl.multiple_of(j * (8 * batch), 8)
        codes = incoming[pl.ds(first, 2 * batch, stride=4), :].astype(jnp.int32)
        row = ((codes >> 6) & 7) * bricks + (codes >> 9)
        index_v[slot] = jnp.clip(row, 0, 7 * bricks - 1)
        index_copy(slot).start()

    sub8 = iota((8, LANES), 0)

    def gather(slot, pair):
        for half in range(2):
            for p in range(LANES):
                rows[half, p : p + 1, :] = table[pl.ds(index_s[slot, 2 * pair + half, p], 1), :]

    def turn():
        for half in range(2):
            cells[half] = rows[half].T

    def weigh(g):
        query = incoming[pl.ds(pl.multiple_of(8 * g, 8), 8), :]
        code = query.astype(jnp.int32)
        results = []
        for half in range(2):
            row = 4 * half
            cy = jnp.broadcast_to((code[row : row + 1] >> 3) & 7, (8, LANES))
            cz = jnp.broadcast_to(code[row : row + 1] & 7, (8, LANES))
            fx = jnp.broadcast_to(query[row + 1 : row + 2], (8, LANES))
            fy = jnp.broadcast_to(query[row + 2 : row + 3], (8, LANES))
            fz = jnp.broadcast_to(query[row + 3 : row + 4], (8, LANES))
            is_y = [cy == y for y in range(7)]
            inter, slope = [], []
            for a in range(2):
                v = [cells[half, 64 * a + 8 * y : 64 * a + 8 * y + 8, :] for y in range(8)]
                low, high = v[0], v[1]
                for y in range(1, 7):
                    low = jnp.where(is_y[y], v[y], low)
                    high = jnp.where(is_y[y], v[y + 1], high)
                inter.append((1.0 - fy) * low + fy * high)
                slope.append(high - low)
            low, high = cz == sub8, cz == sub8 - 1
            weight = jnp.where(low, 1.0 - fz, jnp.where(high, fz, 0.0))
            sign = jnp.where(low, -1.0, jnp.where(high, 1.0, 0.0))
            mixed = (1.0 - fx) * inter[0] + fx * inter[1]
            results += [
                weight * mixed,
                weight * (inter[1] - inter[0]),
                weight * ((1.0 - fx) * slope[0] + fx * slope[1]),
                sign * mixed,
            ]
        for step in (4, 2, 1):
            upper = (sub8 & step) == 0
            count = len(results) // 2
            results = [
                jnp.where(upper, results[i], pltpu.roll(results[i + count], step, 0))
                + jnp.where(upper, pltpu.roll(results[i], 8 - step, 0), results[i + count])
                for i in range(count)
            ]
        answers[pl.ds(pl.multiple_of(8 * g, 8), 8), :] = results[0]

    def step(g, slot, pair):
        weigh(jnp.maximum(g - 2, 0))
        turn()
        if slot is not None:
            gather(slot, pair)

    def finished(j):
        return ((j + 1) * batch + pairs - 2) // pairs - 1

    def segment(j, slot):
        following = j + 1
        source = following // batches

        def prepare():
            if batches == 1 or slot == 1:

                @pl.when(source < devices)
                def _():
                    query_copy(source).wait_recv()

            @pl.when(following < devices * batches)
            def _():
                start_index(following, 1 - slot)

        pl.when(source != 1)(prepare) if batches == 1 or slot == 1 else prepare()
        index_copy(slot).wait()
        for p in range(batch):
            step(j * batch + p, slot, p)
        if batches == 1 or slot == 1:
            pl.when(source == 1)(prepare)
        done = finished(j)

        @pl.when((done > finished(j - 1)) & (done > 1))
        def _():
            answer_copy(done - 1).start()

    def double(i, carry):
        segment(2 * i, 0)
        segment(2 * i + 1, 1)
        return carry

    count = devices * batches
    start_index(0, 0)
    lax.fori_loop(0, count // 2, double, 0)
    step(total, None, None)
    step(total + 1, None, None)
    for k in range(max(finished(count - 1), 1), devices):
        answer_copy(k, k == devices - 1).start()
    landed[0, 0:lines] = answers[0:lines]

    chunks = own_ref.shape[0]
    half = (sub8 >= 4).astype(jnp.int32)

    def collect(slots, first):
        def chunk(c, carry):
            owner = jnp.broadcast_to(own_ref[pl.ds(c, 1), :], (8, LANES))
            rank = jnp.broadcast_to(rank_ref[pl.ds(c, 1), :], (8, LANES))
            lane = rank & (LANES - 1)
            which = (rank >> 7) - half
            value = jnp.zeros((8, LANES), jnp.float32) if first else held[c]
            for k in slots:
                owner_k = ahead(k)
                w = meta_s[c, owner_k] >> 7
                where = pl.ds(4 * w, 8)
                picked = jnp.take_along_axis(
                    landed_last[where, :] if k == devices - 1 else landed[k, where, :], lane, axis=1, mode="promise_in_bounds"
                )
                value = jnp.where((owner == owner_k) & (which == w), picked, value)
            held[c] = value
            return carry

        lax.fori_loop(0, chunks, chunk, 0, unroll=4 if devices <= 8 else 1)

    meta_copy.wait()
    each(devices - 2, lambda k: answer_copy(k + 1).wait_recv(), 8)
    collect(range(devices - 1), True)
    answer_copy(devices - 1, True).wait_recv()
    collect([devices - 1], False)
    dist = held[:, 0, :] + held[:, 4, :]
    hinge = jnp.maximum(margin - dist, 0.0)
    halves = grad_ref.shape[2] // LANES
    quarter = chunks // halves
    for h in range(halves):
        here = hinge[h * quarter : (h + 1) * quarter]
        costs[0, :, h * LANES : (h + 1) * LANES] = jnp.sum(here * here, axis=0, keepdims=True)
    sums = []
    for k in range(1, reps):
        copy = pltpu.make_async_remote_copy(
            src_ref=costs.at[0],
            dst_ref=costs.at[k],
            send_sem=cost_send.at[k],
            recv_sem=cost_recv.at[k],
            device_id=peer_along("rep", reps, k),
            device_id_type=MESH,
        )
        copy.start()
        sums.append(copy)
    for n in range(3):
        grad = -2.0 * hinge * (held[:, 1 + n, :] + held[:, 5 + n, :])
        for h in range(halves):
            grad_ref[n, :, h * LANES : (h + 1) * LANES] = grad[h * quarter : (h + 1) * quarter]

    each(devices - 1, lambda k: query_copy(k + 1).wait_send(), 8)
    each(devices - 2, lambda k: answer_copy(k + 1).wait_send(), 8)
    answer_copy(devices - 1, True).wait_send()
    total_cost = costs[0]
    for k, copy in enumerate(sums):
        copy.wait()
        total_cost = total_cost + costs[k + 1]
    cost_ref[...] = total_cost


def finish_kernel(cost_in, grad_in, cost_out, grad_out, sem):
    copies = [
        pltpu.make_async_copy(grad_in, grad_out, sem.at[0]),
        pltpu.make_async_copy(cost_in, cost_out, sem.at[1]),
    ]
    for copy in copies:
        copy.start()
    for copy in copies:
        copy.wait()


def per_device(field_bricks, owners, bricks, corners, fraction):
    devices = lax.axis_size("map")
    trajectories_here, quarter = owners.shape
    row_count = trajectories_here * quarter
    capacity = 4 * row_count // devices
    tiles = 2 * -(-capacity // (2 * LANES))
    chunks = row_count // LANES
    lines = 4 * tiles
    buffer = jax.ShapeDtypeStruct((devices, lines + 8, LANES), jnp.float32)
    flat = jax.ShapeDtypeStruct((chunks, LANES), jnp.int32)
    vm = pl.BlockSpec(memory_space=VMEM)
    sm = pl.BlockSpec(memory_space=SMEM)
    hbm = pl.BlockSpec(memory_space=pltpu.HBM)
    whole = VMEM((quarter, trajectories_here), jnp.int32)
    outgoing, own, rank, meta = pl.pallas_call(
        functools.partial(dispatch_kernel, devices, tiles),
        out_shape=(buffer, flat, flat, flat),
        in_specs=[hbm] * 4,
        out_specs=(vm,) * 4,
        scratch_shapes=[
            VMEM((chunks, 8, LANES), jnp.float32),
            VMEM((chunks, LANES), jnp.int32),
            SMEM((chunks, LANES), jnp.int32),
            pltpu.SemaphoreType.DMA(()),
            whole, whole, whole,
            VMEM((3, quarter, trajectories_here), jnp.float32),
            pltpu.SemaphoreType.DMA((4,)),
        ],
        compiler_params=pltpu.CompilerParams(vmem_limit_bytes=16 << 20),
        name="dispatch",
    )(*(stay(x) for x in (owners.T, bricks.T, corners.T, fraction.transpose(0, 2, 1))))
    sems = pltpu.SemaphoreType.DMA((devices,))
    reps = lax.axis_size("rep")
    rep_sems = pltpu.SemaphoreType.DMA((reps,))
    batch = batch_of(tiles)
    square = VMEM((2, LANES, LANES), jnp.float32)
    bricks = field_bricks.shape[0]
    cost, waypoint_grad = pl.pallas_call(
        functools.partial(fused_kernel, devices, reps, tiles),
        out_shape=(
            jax.ShapeDtypeStruct((1, trajectories_here), jnp.float32),
            jax.ShapeDtypeStruct((3, quarter, trajectories_here), jnp.float32),
        ),
        in_specs=[vm, hbm, vm, vm, vm],
        out_specs=(vm, vm),
        scratch_shapes=[
            SMEM((chunks, LANES), jnp.int32),
            VMEM((bricks * 7, LANES), jnp.float32),
            VMEM(field_bricks.shape, field_bricks.dtype),
            VMEM((devices * lines, LANES), jnp.float32),
            VMEM((devices * lines, LANES), jnp.float32),
            VMEM((devices - 1, lines + 8, LANES), jnp.float32),
            VMEM((lines + 8, LANES), jnp.float32),
            VMEM((2, 2 * batch, LANES), jnp.int32),
            SMEM((2, 2 * batch, LANES), jnp.int32),
            square, square,
            VMEM((chunks, 8, LANES), jnp.float32),
            VMEM((reps, 1, trajectories_here), jnp.float32),
            pltpu.SemaphoreType.DMA(()),
            pltpu.SemaphoreType.DMA(()),
            pltpu.SemaphoreType.DMA((2,)),
            sems, sems, sems, sems, rep_sems, rep_sems,
        ],
        compiler_params=pltpu.CompilerParams(collective_id=0, has_side_effects=True, vmem_limit_bytes=24 << 20),
        name="fused",
    )(outgoing, stay(field_bricks), own, rank, meta)
    cost, waypoint_grad = pl.pallas_call(
        finish_kernel,
        out_shape=(
            jax.ShapeDtypeStruct(cost.shape, jnp.float32),
            jax.ShapeDtypeStruct(waypoint_grad.shape, jnp.float32),
        ),
        in_specs=[vm] * 2,
        out_specs=(hbm,) * 2,
        scratch_shapes=[pltpu.SemaphoreType.DMA((2,))],
        compiler_params=pltpu.CompilerParams(vmem_limit_bytes=1 << 20),
        name="finish",
    )(cost, waypoint_grad)
    return cost.reshape(trajectories_here), waypoint_grad.transpose(0, 2, 1)


def solution(mesh):
    placed = (
        P("map", None),
        P("map", "rep"),
        P("map", "rep"),
        P("map", "rep"),
        P(None, "map", "rep"),
    )
    return jax.shard_map(
        per_device,
        mesh=mesh,
        in_specs=placed,
        out_specs=(P("map"), P(None, "map", "rep")),
        check_vma=False,
    )
```

time: 42.4 us -> 36.4 us (0.86)
  Pallas kernels: 41.5 us -> 35.5 us
    pallas_call x3 -> x1, Pallas kernels: 36.4 us -> 30.4 us  [per_device(): pl.pallas_call(functools.partial(fused_kernel, devices, reps, tiles), out...]
where the time goes in v2:
time: 36.4 us; the launch traced here: 36.1 us
  Pallas kernels  35.5 us (98%)
  between operations  0.65 us (2%)
    pallas_call x1, Pallas kernels, per_device(): pl.pallas_call(functools.partial(fused_kernel, devices, reps, tiles), out...  30.4 us
    pallas_call x1, Pallas kernels, per_device(): pl.pallas_call(functools.partial(dispatch_kernel, devices, tiles), out_sh...  4.48 us

profile of v2, /device:TPU:0, one launch (start us, length us, event | category | flops | bytes accessed | tf_op | source)
XLA Modules:
  0.0 36.1 jit_solution(4783672378623943860)
XLA Ops:
  0.6 4.5 %dispatch.1 = (f32[8,72,128]{2,1,0:T(8,128)S(1)}, s32[32,128]{1,0:T(8,128)S(1)}, s32[32,128]{1,0:T(8,128)S(1)}, s32[32,128]{1,0:T(8,128)S(1)}) custom-call(s32[16,256]{1,0:T(8,128)} %bitcast.7, s32[16,256]{1,0:T(8,128)} %bitcast.8, s32[16,256]{1,0:T(8,128)} %bitcast.9, f32[3,16,256]{2,1,0:T(8,128)} %bitcast.6), custom_call_target="tpu_custom_call" | custom-call | tf_op jit(solution)/shard_map/dispatch/pallas_call | solution.py:406
  5.1 30.4 %fused.1 = (f32[1,256]{1,0:T(1,128)S(1)}, f32[3,16,256]{2,1,0:T(8,128)S(1)}) custom-call(f32[8,72,128]{2,1,0:T(8,128)S(1)} %get-tuple-element.10.out_in, bf16[2048,512]{1,0:T(8,128)(2,1)} %field_hbm.1, s32[32,128]{1,0:T(8,128)S(1)} %get-tuple-element.11.own_ref, s32[32,128]{1,0:T(8,128)S(1)} %get-tuple-element.12.rank_ref, ...), custom_call_target="tpu_custom_call" | custom-call | tf_op jit(solution)/shard_map/fused/pallas_call | solution.py:429
  35.5 0.6 %finish.1 = (f32[1,256]{1,0:T(1,128)}, f32[3,16,256]{2,1,0:T(8,128)}) custom-call(f32[1,256]{1,0:T(1,128)S(1)} %get-tuple-element.14.cost_in, f32[3,16,256]{2,1,0:T(8,128)S(1)} %get-tuple-element.15.grad_in), custom_call_target="tpu_custom_call" | custom-call | tf_op jit(solution)/shard_map/finish/pallas_call | solution.py:458

commit v3 on v2

--- a/solution.py
+++ b/solution.py
@@ -39,8 +39,8 @@
 
 
 def dispatch_kernel(
-    devices, tiles, owners_hbm, bricks_hbm, corners_hbm, frac_hbm,
-    out_ref, own_ref, rank_ref, meta_ref,
+    devices, tiles, owners_hbm, bricks_hbm, corners_hbm, frac_hbm, field_hbm,
+    out_ref, own_ref, rank_ref, meta_ref, field_ref,
     data_ref, pos_ref, meta_s, sem, owners_ref, bricks_ref, corners_ref, frac_ref, load_sem,
 ):
     loads = [
@@ -52,6 +52,8 @@
     ]
     for load in loads:
         load.start()
+    field_load = pltpu.make_async_copy(field_hbm, field_ref, load_sem.at[4])
+    field_load.start()
     out_ref[...] = jnp.zeros_like(out_ref)
     for load in loads:
         load.wait()
@@ -125,6 +127,7 @@
         return carry
 
     lax.fori_loop(0, chunks, place_chunk, 0, unroll=4 if devices <= 8 else 1)
+    field_load.wait()
 
 
 def greet(peers):
@@ -143,19 +146,18 @@
 
 
 def fused_kernel(
-    devices, reps, tiles, out_in, field_hbm, own_ref, rank_ref, meta_ref, cost_ref, grad_ref,
-    meta_s, table, field_ref, incoming, answers, landed, landed_last, index_v, index_s, rows, cells, held, costs,
-    field_sem, meta_sem, index_sem, query_send, query_recv, answer_send, answer_recv, cost_send, cost_recv,
+    devices, reps, tiles, out_in, field_ref, own_ref, rank_ref, meta_ref, cost_ref, grad_ref,
+    meta_s, table, incoming, answers, landed, landed_last, index_v, index_s, cells, held, costs,
+    meta_sem, index_sem, query_send, query_recv, answer_send, answer_recv, cost_send, cost_recv,
 ):
     lines = 4 * tiles
     pairs = tiles // 2
     total = devices * pairs
     batch = batch_of(tiles)
     batches = pairs // batch
+    rooms = 2 if batch % 2 == 0 else 1
     bricks = field_ref.shape[0]
     me = lax.axis_index("map")
-    load = pltpu.make_async_copy(field_hbm, field_ref, field_sem)
-    load.start()
     meta_copy = pltpu.make_async_copy(meta_ref, meta_s, meta_sem)
     meta_copy.start()
     wait_peers = greet(
@@ -163,34 +165,54 @@
         + [peer_along("rep", reps, k) for k in range(1, reps)]
     )
 
-    def ahead(k):
-        return lax.rem(me + k, devices)
-
-    def behind(k):
-        return lax.rem(me + devices - k, devices)
-
-    def query_copy(k):
+    head = pairs // 2 // batch * batch
+
+    def hop(j):
+        if isinstance(j, int):
+            return 2 if j == devices - 1 else j + (j >= 2)
+        return jnp.where(j == devices - 1, 2, j + (j >= 2).astype(jnp.int32))
+
+    if devices & (devices - 1) == 0:
+
+        def asked(j):
+            return lax.bitwise_xor(me, jnp.int32(hop(j)))
+
+        asker = asked
+    else:
+
+        def asked(j):
+            return lax.rem(me + j, devices)
+
+        def asker(j):
+            return lax.rem(me + devices - j, devices)
+
+    def slot_rows(j):
+        return pl.ds(pl.multiple_of(8 * (head + (j - 1) * pairs), 8), lines)
+
+    def query_copy(j):
         return pltpu.make_async_remote_copy(
-            src_ref=out_in.at[ahead(k), pl.ds(0, lines)],
-            dst_ref=incoming.at[pl.ds(pl.multiple_of(k * lines, 8), lines)],
-            send_sem=query_send.at[k],
-            recv_sem=query_recv.at[k],
-            device_id={"map": ahead(k)},
+            src_ref=out_in.at[asked(j), pl.ds(0, lines)],
+            dst_ref=incoming.at[slot_rows(j)],
+            send_sem=query_send.at[j],
+            recv_sem=query_recv.at[j],
+            device_id={"map": asked(j)},
             device_id_type=MESH,
         )
 
-    def answer_copy(k, last=False):
+    def answer_copy(j, last=False):
         return pltpu.make_async_remote_copy(
-            src_ref=answers.at[pl.ds(pl.multiple_of(k * lines, 8), lines)],
-            dst_ref=(landed_last if last else landed.at[k]).at[pl.ds(0, lines)],
-            send_sem=answer_send.at[k],
-            recv_sem=answer_recv.at[k],
-            device_id={"map": behind(k)},
+            src_ref=answers.at[slot_rows(j)],
+            dst_ref=(landed_last if last else landed.at[j]).at[pl.ds(0, lines)],
+            send_sem=answer_send.at[j],
+            recv_sem=answer_recv.at[j],
+            device_id={"map": asker(j)},
             device_id_type=MESH,
         )
 
-    incoming[0:lines] = out_in[me, 0:lines]
-    rows[...] = jnp.zeros_like(rows)
+    tail_row = 8 * (total - pairs + head)
+    if head:
+        incoming[0 : 8 * head] = out_in[me, 0 : 8 * head]
+    incoming[tail_row:] = out_in[me, 8 * head : lines]
     cells[...] = jnp.zeros_like(cells)
 
     def build(g, carry):
@@ -201,7 +223,6 @@
 
     wait_peers()
     each(devices - 1, lambda k: query_copy(k + 1).start(), 8)
-    load.wait()
     lax.fori_loop(0, bricks // 16, build, 0, unroll=32)
 
     def index_copy(slot):
@@ -218,14 +239,10 @@
 
     def gather(slot, pair):
         for half in range(2):
-            for p in range(LANES):
-                rows[half, p : p + 1, :] = table[pl.ds(index_s[slot, 2 * pair + half, p], 1), :]
-
-    def turn():
-        for half in range(2):
-            cells[half] = rows[half].T
-
-    def weigh(g):
+            picked = [table[pl.ds(index_s[slot, 2 * pair + half, p], 1), :] for p in range(LANES)]
+            cells[pair % rooms, half] = jnp.concatenate(picked, axis=0).T
+
+    def weigh(g, now):
         query = incoming[pl.ds(pl.multiple_of(8 * g, 8), 8), :]
         code = query.astype(jnp.int32)
         results = []
@@ -239,7 +256,7 @@
             is_y = [cy == y for y in range(7)]
             inter, slope = [], []
             for a in range(2):
-                v = [cells[half, 64 * a + 8 * y : 64 * a + 8 * y + 8, :] for y in range(8)]
+                v = [cells[now, half, 64 * a + 8 * y : 64 * a + 8 * y + 8, :] for y in range(8)]
                 low, high = v[0], v[1]
                 for y in range(1, 7):
                     low = jnp.where(is_y[y], v[y], low)
@@ -267,54 +284,82 @@
         answers[pl.ds(pl.multiple_of(8 * g, 8), 8), :] = results[0]
 
     def step(g, slot, pair):
-        weigh(jnp.maximum(g - 2, 0))
-        turn()
+        weigh(jnp.maximum(g - 1, 0), (pair + 1) % rooms)
         if slot is not None:
             gather(slot, pair)
 
+    head_batches = head // batch
+    count = devices * batches
+    remote_end = head_batches + (devices - 1) * batches
+
     def finished(j):
-        return ((j + 1) * batch + pairs - 2) // pairs - 1
-
-    def segment(j, slot):
-        following = j + 1
-        source = following // batches
-
-        def prepare():
-            if batches == 1 or slot == 1:
-
-                @pl.when(source < devices)
-                def _():
-                    query_copy(source).wait_recv()
-
-            @pl.when(following < devices * batches)
+        return ((j + 1) * batch - 1 - head + pairs) // pairs - 1
+
+    def prepare(i, slot):
+        following = 2 * i + slot + 1
+        if batches == 2:
+            fresh, origin = (slot == 0, i + 1)
+        elif batches == 1:
+            fresh, origin = (True, following + 1)
+        else:
+            past = following - head_batches + batches
+            origin = past // batches
+            fresh = (past % batches == 0) & (past >= batches)
+        if fresh is not False:
+
+            @pl.when((origin < devices) & fresh)
             def _():
-                start_index(following, 1 - slot)
-
-        pl.when(source != 1)(prepare) if batches == 1 or slot == 1 else prepare()
+                query_copy(origin).wait_recv()
+
+        @pl.when(following < count)
+        def _():
+            start_index(following, 1 - slot)
+
+    def segment(i, slot):
+        j = 2 * i + slot
+        if head_batches:
+            late = j + 1 == head_batches
+            pl.when(jnp.logical_not(late))(lambda: prepare(i, slot))
+        else:
+            prepare(i, slot)
         index_copy(slot).wait()
         for p in range(batch):
             step(j * batch + p, slot, p)
-        if batches == 1 or slot == 1:
-            pl.when(source == 1)(prepare)
-        done = finished(j)
-
-        @pl.when((done > finished(j - 1)) & (done > 1))
-        def _():
-            answer_copy(done - 1).start()
+        if head_batches:
+            pl.when(late)(lambda: prepare(i, slot))
+        if batches == 2:
+            done, ready = i, slot == 1
+        elif batches == 1:
+            done, ready = j, True
+        else:
+            done = finished(j)
+            ready = done > finished(j - 1)
+        if ready is not False:
+
+            @pl.when(ready & (done > 0) & (done < devices - 1))
+            def _():
+                answer_copy(done).start()
 
     def double(i, carry):
-        segment(2 * i, 0)
-        segment(2 * i + 1, 1)
+        segment(i, 0)
+        segment(i, 1)
         return carry
 
-    count = devices * batches
+    if head_batches == 0:
+        query_copy(1).wait_recv()
     start_index(0, 0)
     lax.fori_loop(0, count // 2, double, 0)
-    step(total, None, None)
-    step(total + 1, None, None)
-    for k in range(max(finished(count - 1), 1), devices):
-        answer_copy(k, k == devices - 1).start()
-    landed[0, 0:lines] = answers[0:lines]
+    early = min(max(finished(count - 1), 0), devices - 2)
+    sent_last = finished(count - 1) >= devices - 1
+    if sent_last:
+        answer_copy(devices - 1, True).start()
+    step(total, None, 0)
+    if not sent_last:
+        for k in range(early + 1, devices):
+            answer_copy(k, k == devices - 1).start()
+    if head:
+        landed[0, 0 : 8 * head] = answers[0 : 8 * head]
+    landed[0, 8 * head : lines] = answers[tail_row:]
 
     chunks = own_ref.shape[0]
     half = (sub8 >= 4).astype(jnp.int32)
@@ -327,7 +372,7 @@
             which = (rank >> 7) - half
             value = jnp.zeros((8, LANES), jnp.float32) if first else held[c]
             for k in slots:
-                owner_k = ahead(k)
+                owner_k = asked(k) if k else me
                 w = meta_s[c, owner_k] >> 7
                 where = pl.ds(4 * w, 8)
                 picked = jnp.take_along_axis(
@@ -403,11 +448,11 @@
     sm = pl.BlockSpec(memory_space=SMEM)
     hbm = pl.BlockSpec(memory_space=pltpu.HBM)
     whole = VMEM((quarter, trajectories_here), jnp.int32)
-    outgoing, own, rank, meta = pl.pallas_call(
+    outgoing, own, rank, meta, field = pl.pallas_call(
         functools.partial(dispatch_kernel, devices, tiles),
-        out_shape=(buffer, flat, flat, flat),
-        in_specs=[hbm] * 4,
-        out_specs=(vm,) * 4,
+        out_shape=(buffer, flat, flat, flat, jax.ShapeDtypeStruct(field_bricks.shape, field_bricks.dtype)),
+        in_specs=[hbm] * 5,
+        out_specs=(vm,) * 5,
         scratch_shapes=[
             VMEM((chunks, 8, LANES), jnp.float32),
             VMEM((chunks, LANES), jnp.int32),
@@ -415,16 +460,16 @@
             pltpu.SemaphoreType.DMA(()),
             whole, whole, whole,
             VMEM((3, quarter, trajectories_here), jnp.float32),
-            pltpu.SemaphoreType.DMA((4,)),
+            pltpu.SemaphoreType.DMA((5,)),
         ],
         compiler_params=pltpu.CompilerParams(vmem_limit_bytes=16 << 20),
         name="dispatch",
-    )(*(stay(x) for x in (owners.T, bricks.T, corners.T, fraction.transpose(0, 2, 1))))
+    )(*(stay(x) for x in (owners.T, bricks.T, corners.T, fraction.transpose(0, 2, 1), field_bricks)))
     sems = pltpu.SemaphoreType.DMA((devices,))
     reps = lax.axis_size("rep")
     rep_sems = pltpu.SemaphoreType.DMA((reps,))
     batch = batch_of(tiles)
-    square = VMEM((2, LANES, LANES), jnp.float32)
+    square = VMEM((2 if batch % 2 == 0 else 1, 2, LANES, LANES), jnp.float32)
     bricks = field_bricks.shape[0]
     cost, waypoint_grad = pl.pallas_call(
         functools.partial(fused_kernel, devices, reps, tiles),
@@ -432,29 +477,27 @@
             jax.ShapeDtypeStruct((1, trajectories_here), jnp.float32),
             jax.ShapeDtypeStruct((3, quarter, trajectories_here), jnp.float32),
         ),
-        in_specs=[vm, hbm, vm, vm, vm],
+        in_specs=[vm] * 5,
         out_specs=(vm, vm),
         scratch_shapes=[
             SMEM((chunks, LANES), jnp.int32),
             VMEM((bricks * 7, LANES), jnp.float32),
-            VMEM(field_bricks.shape, field_bricks.dtype),
             VMEM((devices * lines, LANES), jnp.float32),
             VMEM((devices * lines, LANES), jnp.float32),
             VMEM((devices - 1, lines + 8, LANES), jnp.float32),
             VMEM((lines + 8, LANES), jnp.float32),
             VMEM((2, 2 * batch, LANES), jnp.int32),
             SMEM((2, 2 * batch, LANES), jnp.int32),
-            square, square,
+            square,
             VMEM((chunks, 8, LANES), jnp.float32),
             VMEM((reps, 1, trajectories_here), jnp.float32),
-            pltpu.SemaphoreType.DMA(()),
             pltpu.SemaphoreType.DMA(()),
             pltpu.SemaphoreType.DMA((2,)),
             sems, sems, sems, sems, rep_sems, rep_sems,
         ],
         compiler_params=pltpu.CompilerParams(collective_id=0, has_side_effects=True, vmem_limit_bytes=24 << 20),
         name="fused",
-    )(outgoing, stay(field_bricks), own, rank, meta)
+    )(outgoing, field, own, rank, meta)
     cost, waypoint_grad = pl.pallas_call(
         finish_kernel,
         out_shape=(

time: 36.4 us -> 33.7 us (0.926)
  Pallas kernels: 35.5 us -> 32.8 us
    pallas_call x1, Pallas kernels: 30.4 us -> 27.6 us  [per_device(): pl.pallas_call(functools.partial(fused_kernel, devices, reps, tiles), out...]
where the time goes in v3:
time: 33.7 us; the launch traced here: 33.4 us
  Pallas kernels  32.8 us (97%)
  between operations  0.65 us (2%)
    pallas_call x1, Pallas kernels, per_device(): pl.pallas_call(functools.partial(fused_kernel, devices, reps, tiles), out...  27.6 us
    pallas_call x1, Pallas kernels, per_device(): pl.pallas_call(functools.partial(dispatch_kernel, devices, tiles), out_sh...  4.49 us

profile of v3, /device:TPU:0, one launch (start us, length us, event | category | flops | bytes accessed | tf_op | source)
XLA Modules:
  0.0 33.4 jit_solution(5675499231410820132)
XLA Ops:
  0.6 4.5 %dispatch.1 = (f32[8,72,128]{2,1,0:T(8,128)S(1)}, s32[32,128]{1,0:T(8,128)S(1)}, s32[32,128]{1,0:T(8,128)S(1)}, s32[32,128]{1,0:T(8,128)S(1)}, bf16[2048,512]{1,0:T(8,128)(2,1)S(1)}) custom-call(s32[16,256]{1,0:T(8,128)} %bitcast.7, s32[16,256]{1,0:T(8,128)} %bitcast.8, s32[16,256]{1,0:T(8,128)} %bitcast.9, f32[3,16,256]{2,1,0:T(8,128)} %bitcast.6, ...), custom_call_target="tpu_custom_call" | custom-call | tf_op jit(solution)/shard_map/dispatch/pallas_call | solution.py:451
  5.1 27.6 %fused.1 = (f32[1,256]{1,0:T(1,128)S(1)}, f32[3,16,256]{2,1,0:T(8,128)S(1)}) custom-call(f32[8,72,128]{2,1,0:T(8,128)S(1)} %get-tuple-element.11.out_in, bf16[2048,512]{1,0:T(8,128)(2,1)S(1)} %get-tuple-element.12.field_ref, s32[32,128]{1,0:T(8,128)S(1)} %get-tuple-element.13.own_ref, s32[32,128]{1,0:T(8,128)S(1)} %get-tuple-element.14.rank_ref, ...), custom_call_target="tpu_custom_call" | custom-call | tf_op jit(solution)/shard_map/fused/pallas_call | solution.py:474
  32.8 0.6 %finish.1 = (f32[1,256]{1,0:T(1,128)}, f32[3,16,256]{2,1,0:T(8,128)}) custom-call(f32[1,256]{1,0:T(1,128)S(1)} %get-tuple-element.16.cost_in, f32[3,16,256]{2,1,0:T(8,128)S(1)} %get-tuple-element.17.grad_in), custom_call_target="tpu_custom_call" | custom-call | tf_op jit(solution)/shard_map/finish/pallas_call | solution.py:501

commit v4 on v3

--- a/solution.py
+++ b/solution.py
@@ -41,7 +41,7 @@
 def dispatch_kernel(
     devices, tiles, owners_hbm, bricks_hbm, corners_hbm, frac_hbm, field_hbm,
     out_ref, own_ref, rank_ref, meta_ref, field_ref,
-    data_ref, pos_ref, meta_s, sem, owners_ref, bricks_ref, corners_ref, frac_ref, load_sem,
+    data_ref, pos_ref, meta_s, sem, owners_ref, bricks_ref, corners_ref, frac_ref, load_sem, *piles,
 ):
     loads = [
         pltpu.make_async_copy(source, target, load_sem.at[i])
@@ -54,7 +54,8 @@
         load.start()
     field_load = pltpu.make_async_copy(field_hbm, field_ref, load_sem.at[4])
     field_load.start()
-    out_ref[...] = jnp.zeros_like(out_ref)
+    for pile in piles or (out_ref,):
+        pile[...] = jnp.zeros_like(pile)
     for load in loads:
         load.wait()
     own = lanes_of(owners_ref[...])
@@ -92,6 +93,10 @@
         meta = jnp.where(lane == o, off.astype(jnp.int32), meta)
         turn = (off - start).astype(jnp.int32) & (LANES - 1)
         meta = jnp.where(lane == devices + o, turn, meta)
+        if piles:
+            whole = off.astype(jnp.int32)
+            meta = jnp.where(lane == 2 * devices + o, 4 * (whole >> 7), meta)
+            meta = jnp.where(lane == 3 * devices + o, whole & (LANES - 1), meta)
         start = start + total
     rank_ref[...] = rank.astype(jnp.int32)
     pos_ref[...] = pos.astype(jnp.int32)
@@ -123,10 +128,19 @@
             keep = (sub8 < 4) & (lane8 < (off & (LANES - 1)))
             out_ref[o, where_to, :] = jnp.where(keep, out_ref[o, where_to, :], turned)
 
-        each(devices, place, 8)
+        if piles:
+            for o, pile in enumerate(piles):
+                where_to = pl.ds(meta_s[c, 2 * devices + o], 8)
+                turned = pltpu.roll(row, meta_s[c, devices + o], 1)
+                keep = (sub8 < 4) & (lane8 < meta_s[c, 3 * devices + o])
+                pile[where_to, :] = jnp.where(keep, pile[where_to, :], turned)
+        else:
+            each(devices, place, 8)
         return carry
 
-    lax.fori_loop(0, chunks, place_chunk, 0, unroll=4 if devices <= 8 else 1)
+    lax.fori_loop(0, chunks, place_chunk, 0, unroll=8 if piles else 1)
+    for o, pile in enumerate(piles):
+        out_ref[o] = pile[...]
     field_load.wait()
 
 
@@ -147,7 +161,7 @@
 
 def fused_kernel(
     devices, reps, tiles, out_in, field_ref, own_ref, rank_ref, meta_ref, cost_ref, grad_ref,
-    meta_s, table, incoming, answers, landed, landed_last, index_v, index_s, cells, held, costs,
+    meta_s, table, incoming, answers, landed, landed_late, index_v, index_s, cells, held, costs,
     meta_sem, index_sem, query_send, query_recv, answer_send, answer_recv, cost_send, cost_recv,
 ):
     lines = 4 * tiles
@@ -199,10 +213,12 @@
             device_id_type=MESH,
         )
 
-    def answer_copy(j, last=False):
+    keep = devices - 2
+
+    def answer_copy(j, late=False):
         return pltpu.make_async_remote_copy(
             src_ref=answers.at[slot_rows(j)],
-            dst_ref=(landed_last if last else landed.at[j]).at[pl.ds(0, lines)],
+            dst_ref=(landed_late.at[j - keep] if late else landed.at[j]).at[pl.ds(0, lines)],
             send_sem=answer_send.at[j],
             recv_sem=answer_recv.at[j],
             device_id={"map": asker(j)},
@@ -315,7 +331,7 @@
         def _():
             start_index(following, 1 - slot)
 
-    def segment(i, slot):
+    def segment(i, slot, final=False):
         j = 2 * i + slot
         if head_batches:
             late = j + 1 == head_batches
@@ -325,6 +341,8 @@
         index_copy(slot).wait()
         for p in range(batch):
             step(j * batch + p, slot, p)
+            if final and p == min(1, batch - 1):
+                answer_copy(devices - 1, True).start()
         if head_batches:
             pl.when(late)(lambda: prepare(i, slot))
         if batches == 2:
@@ -334,11 +352,15 @@
         else:
             done = finished(j)
             ready = done > finished(j - 1)
-        if ready is not False:
-
-            @pl.when(ready & (done > 0) & (done < devices - 1))
+        if ready is not False and not final:
+
+            @pl.when(ready & (done > 0) & (done < keep))
             def _():
                 answer_copy(done).start()
+
+            @pl.when(ready & (done == keep))
+            def _():
+                answer_copy(keep, True).start()
 
     def double(i, carry):
         segment(i, 0)
@@ -348,15 +370,10 @@
     if head_batches == 0:
         query_copy(1).wait_recv()
     start_index(0, 0)
-    lax.fori_loop(0, count // 2, double, 0)
-    early = min(max(finished(count - 1), 0), devices - 2)
-    sent_last = finished(count - 1) >= devices - 1
-    if sent_last:
-        answer_copy(devices - 1, True).start()
+    lax.fori_loop(0, count // 2 - 1, double, 0)
+    segment(jnp.int32(count // 2 - 1), 0)
+    segment(jnp.int32(count // 2 - 1), 1, True)
     step(total, None, 0)
-    if not sent_last:
-        for k in range(early + 1, devices):
-            answer_copy(k, k == devices - 1).start()
     if head:
         landed[0, 0 : 8 * head] = answers[0 : 8 * head]
     landed[0, 8 * head : lines] = answers[tail_row:]
@@ -364,7 +381,7 @@
     chunks = own_ref.shape[0]
     half = (sub8 >= 4).astype(jnp.int32)
 
-    def collect(slots, first):
+    def collect(slots, first, unroll):
         def chunk(c, carry):
             owner = jnp.broadcast_to(own_ref[pl.ds(c, 1), :], (8, LANES))
             rank = jnp.broadcast_to(rank_ref[pl.ds(c, 1), :], (8, LANES))
@@ -376,19 +393,20 @@
                 w = meta_s[c, owner_k] >> 7
                 where = pl.ds(4 * w, 8)
                 picked = jnp.take_along_axis(
-                    landed_last[where, :] if k == devices - 1 else landed[k, where, :], lane, axis=1, mode="promise_in_bounds"
+                    landed_late[k - keep, where, :] if k >= keep else landed[k, where, :], lane, axis=1, mode="promise_in_bounds"
                 )
                 value = jnp.where((owner == owner_k) & (which == w), picked, value)
             held[c] = value
             return carry
 
-        lax.fori_loop(0, chunks, chunk, 0, unroll=4 if devices <= 8 else 1)
+        lax.fori_loop(0, chunks, chunk, 0, unroll=unroll if devices <= 8 else 1)
 
     meta_copy.wait()
-    each(devices - 2, lambda k: answer_copy(k + 1).wait_recv(), 8)
-    collect(range(devices - 1), True)
-    answer_copy(devices - 1, True).wait_recv()
-    collect([devices - 1], False)
+    each(keep - 1, lambda k: answer_copy(k + 1).wait_recv(), 8)
+    collect(range(keep), True, 8)
+    for k in (keep, keep + 1):
+        answer_copy(k, True).wait_recv()
+    collect((keep, keep + 1), False, 16)
     dist = held[:, 0, :] + held[:, 4, :]
     hinge = jnp.maximum(margin - dist, 0.0)
     halves = grad_ref.shape[2] // LANES
@@ -414,8 +432,9 @@
             grad_ref[n, :, h * LANES : (h + 1) * LANES] = grad[h * quarter : (h + 1) * quarter]
 
     each(devices - 1, lambda k: query_copy(k + 1).wait_send(), 8)
-    each(devices - 2, lambda k: answer_copy(k + 1).wait_send(), 8)
-    answer_copy(devices - 1, True).wait_send()
+    each(keep - 1, lambda k: answer_copy(k + 1).wait_send(), 8)
+    for k in (keep, keep + 1):
+        answer_copy(k, True).wait_send()
     total_cost = costs[0]
     for k, copy in enumerate(sums):
         copy.wait()
@@ -461,7 +480,8 @@
             whole, whole, whole,
             VMEM((3, quarter, trajectories_here), jnp.float32),
             pltpu.SemaphoreType.DMA((5,)),
-        ],
+        ]
+        + [VMEM((lines + 8, LANES), jnp.float32)] * (devices if devices <= 8 else 0),
         compiler_params=pltpu.CompilerParams(vmem_limit_bytes=16 << 20),
         name="dispatch",
     )(*(stay(x) for x in (owners.T, bricks.T, corners.T, fraction.transpose(0, 2, 1), field_bricks)))
@@ -484,8 +504,8 @@
             VMEM((bricks * 7, LANES), jnp.float32),
             VMEM((devices * lines, LANES), jnp.float32),
             VMEM((devices * lines, LANES), jnp.float32),
-            VMEM((devices - 1, lines + 8, LANES), jnp.float32),
-            VMEM((lines + 8, LANES), jnp.float32),
+            VMEM((devices - 2, lines + 8, LANES), jnp.float32),
+            VMEM((2, lines + 8, LANES), jnp.float32),
             VMEM((2, 2 * batch, LANES), jnp.int32),
             SMEM((2, 2 * batch, LANES), jnp.int32),
             square,

time: 33.7 us -> 31.4 us (0.932)
  Pallas kernels: 32.8 us -> 30.6 us
    pallas_call x1, Pallas kernels: 27.6 us -> 26.3 us  [per_device(): pl.pallas_call(functools.partial(fused_kernel, devices, reps, tiles), out...]
    pallas_call x1, Pallas kernels: 4.49 us -> 3.65 us  [per_device(): pl.pallas_call(functools.partial(dispatch_kernel, devices, tiles), out_sh...]
where the time goes in v4:
time: 31.4 us; the launch traced here: 31.2 us
  Pallas kernels  30.6 us (97%)
  between operations  0.65 us (2%)
    pallas_call x1, Pallas kernels, per_device(): pl.pallas_call(functools.partial(fused_kernel, devices, reps, tiles), out...  26.3 us
    pallas_call x1, Pallas kernels, per_device(): pl.pallas_call(functools.partial(dispatch_kernel, devices, tiles), out_sh...  3.65 us
    pallas_call x1, Pallas kernels, per_device(): pl.pallas_call(finish_kernel, out_shape=(jax.ShapeDtypeStruct(cost.shape,...  0.64 us

profile of v4, /device:TPU:0, one launch (start us, length us, event | category | flops | bytes accessed | tf_op | source)
XLA Modules:
  0.0 31.2 jit_solution(13983071034179195284)
XLA Ops:
  0.6 3.6 %dispatch.1 = (f32[8,72,128]{2,1,0:T(8,128)S(1)}, s32[32,128]{1,0:T(8,128)S(1)}, s32[32,128]{1,0:T(8,128)S(1)}, s32[32,128]{1,0:T(8,128)S(1)}, bf16[2048,512]{1,0:T(8,128)(2,1)S(1)}) custom-call(s32[16,256]{1,0:T(8,128)} %bitcast.7, s32[16,256]{1,0:T(8,128)} %bitcast.8, s32[16,256]{1,0:T(8,128)} %bitcast.9, f32[3,16,256]{2,1,0:T(8,128)} %bitcast.6, ...), custom_call_target="tpu_custom_call" | custom-call | tf_op jit(solution)/shard_map/dispatch/pallas_call | solution.py:470
  4.3 26.3 %fused.1 = (f32[1,256]{1,0:T(1,128)S(1)}, f32[3,16,256]{2,1,0:T(8,128)S(1)}) custom-call(f32[8,72,128]{2,1,0:T(8,128)S(1)} %get-tuple-element.11.out_in, bf16[2048,512]{1,0:T(8,128)(2,1)S(1)} %get-tuple-element.12.field_ref, s32[32,128]{1,0:T(8,128)S(1)} %get-tuple-element.13.own_ref, s32[32,128]{1,0:T(8,128)S(1)} %get-tuple-element.14.rank_ref, ...), custom_call_target="tpu_custom_call" | custom-call | tf_op jit(solution)/shard_map/fused/pallas_call | solution.py:494
  30.6 0.6 %finish.1 = (f32[1,256]{1,0:T(1,128)}, f32[3,16,256]{2,1,0:T(8,128)}) custom-call(f32[1,256]{1,0:T(1,128)S(1)} %get-tuple-element.16.cost_in, f32[3,16,256]{2,1,0:T(8,128)S(1)} %get-tuple-element.17.grad_in), custom_call_target="tpu_custom_call" | custom-call | tf_op jit(solution)/shard_map/finish/pallas_call | solution.py:521

commit v5 on v4

--- a/solution.py
+++ b/solution.py
@@ -82,12 +82,31 @@
     pos = jnp.zeros((chunks, LANES), jnp.float32)
     start = jnp.zeros((chunks, LANES), jnp.float32)
     meta = jnp.zeros((chunks, LANES), jnp.int32)
+    if piles:
+        stacked = jnp.concatenate(
+            [(own == o).astype(jnp.float32) for o in range(devices)], axis=0
+        ).astype(jnp.bfloat16)
+        both = jnp.dot(
+            stacked, jnp.concatenate([upper, ones], axis=1), preferred_element_type=jnp.float32
+        )
+        totals = both[:, LANES:]
+        size = devices * chunks
+        down, across = iota((size, size), 0), iota((size, size), 1)
+        same = (down // chunks == across // chunks) & (down > across)
+        offs = jnp.dot(
+            same.astype(jnp.float32).astype(jnp.bfloat16), totals.astype(jnp.bfloat16),
+            preferred_element_type=jnp.float32,
+        )
     for o in range(devices):
         member = own == o
-        m16 = member.astype(jnp.float32).astype(jnp.bfloat16)
-        incl = jnp.dot(m16, upper, preferred_element_type=jnp.float32) - 1.0
-        total = jnp.dot(m16, ones, preferred_element_type=jnp.float32)
-        off = jnp.dot(before, total.astype(jnp.bfloat16), preferred_element_type=jnp.float32)
+        if piles:
+            here = slice(o * chunks, (o + 1) * chunks)
+            incl, total, off = both[here, :LANES] - 1.0, totals[here], offs[here]
+        else:
+            m16 = member.astype(jnp.float32).astype(jnp.bfloat16)
+            incl = jnp.dot(m16, upper, preferred_element_type=jnp.float32) - 1.0
+            total = jnp.dot(m16, ones, preferred_element_type=jnp.float32)
+            off = jnp.dot(before, total.astype(jnp.bfloat16), preferred_element_type=jnp.float32)
         rank = jnp.where(member, incl + off, rank)
         pos = jnp.where(member, incl + start, pos)
         meta = jnp.where(lane == o, off.astype(jnp.int32), meta)
@@ -138,7 +157,7 @@
             each(devices, place, 8)
         return carry
 
-    lax.fori_loop(0, chunks, place_chunk, 0, unroll=8 if piles else 1)
+    lax.fori_loop(0, chunks, place_chunk, 0, unroll=16 if piles else 1)
     for o, pile in enumerate(piles):
         out_ref[o] = pile[...]
     field_load.wait()
@@ -239,7 +258,7 @@
 
     wait_peers()
     each(devices - 1, lambda k: query_copy(k + 1).start(), 8)
-    lax.fori_loop(0, bricks // 16, build, 0, unroll=32)
+    lax.fori_loop(0, bricks // 16, build, 0, unroll=64)
 
     def index_copy(slot):
         return pltpu.make_async_copy(index_v.at[slot], index_s.at[slot], index_sem.at[slot])
@@ -403,10 +422,10 @@
 
     meta_copy.wait()
     each(keep - 1, lambda k: answer_copy(k + 1).wait_recv(), 8)
-    collect(range(keep), True, 8)
+    collect(range(keep), True, 16)
     for k in (keep, keep + 1):
         answer_copy(k, True).wait_recv()
-    collect((keep, keep + 1), False, 16)
+    collect((keep, keep + 1), False, 32)
     dist = held[:, 0, :] + held[:, 4, :]
     hinge = jnp.maximum(margin - dist, 0.0)
     halves = grad_ref.shape[2] // LANES

time: 31.4 us -> 30.5 us (0.971)
  Pallas kernels: 30.6 us -> 29.6 us
    pallas_call x1, Pallas kernels: 3.65 us -> 2.79 us  [per_device(): pl.pallas_call(functools.partial(dispatch_kernel, devices, tiles), out_sh...]
where the time goes in v5:
time: 30.5 us; the launch traced here: 30.2 us
  Pallas kernels  29.6 us (97%)
  between operations  0.65 us (2%)
    pallas_call x1, Pallas kernels, per_device(): pl.pallas_call(functools.partial(fused_kernel, devices, reps, tiles), out...  26.2 us
    pallas_call x1, Pallas kernels, per_device(): pl.pallas_call(functools.partial(dispatch_kernel, devices, tiles), out_sh...  2.79 us
    pallas_call x1, Pallas kernels, per_device(): pl.pallas_call(finish_kernel, out_shape=(jax.ShapeDtypeStruct(cost.shape,...  0.64 us

profile of v5, /device:TPU:0, one launch (start us, length us, event | category | flops | bytes accessed | tf_op | source)
XLA Modules:
  0.0 30.2 jit_solution(16521679560133180394)
XLA Ops:
  0.6 2.8 %dispatch.1 = (f32[8,72,128]{2,1,0:T(8,128)S(1)}, s32[32,128]{1,0:T(8,128)S(1)}, s32[32,128]{1,0:T(8,128)S(1)}, s32[32,128]{1,0:T(8,128)S(1)}, bf16[2048,512]{1,0:T(8,128)(2,1)S(1)}) custom-call(s32[16,256]{1,0:T(8,128)} %bitcast.7, s32[16,256]{1,0:T(8,128)} %bitcast.8, s32[16,256]{1,0:T(8,128)} %bitcast.9, f32[3,16,256]{2,1,0:T(8,128)} %bitcast.6, ...), custom_call_target="tpu_custom_call" | custom-call | tf_op jit(solution)/shard_map/dispatch/pallas_call | solution.py:489
  3.4 26.2 %fused.1 = (f32[1,256]{1,0:T(1,128)S(1)}, f32[3,16,256]{2,1,0:T(8,128)S(1)}) custom-call(f32[8,72,128]{2,1,0:T(8,128)S(1)} %get-tuple-element.11.out_in, bf16[2048,512]{1,0:T(8,128)(2,1)S(1)} %get-tuple-element.12.field_ref, s32[32,128]{1,0:T(8,128)S(1)} %get-tuple-element.13.own_ref, s32[32,128]{1,0:T(8,128)S(1)} %get-tuple-element.14.rank_ref, ...), custom_call_target="tpu_custom_call" | custom-call | tf_op jit(solution)/shard_map/fused/pallas_call | solution.py:513
  29.6 0.6 %finish.1 = (f32[1,256]{1,0:T(1,128)}, f32[3,16,256]{2,1,0:T(8,128)}) custom-call(f32[1,256]{1,0:T(1,128)S(1)} %get-tuple-element.16.cost_in, f32[3,16,256]{2,1,0:T(8,128)S(1)} %get-tuple-element.17.grad_in), custom_call_target="tpu_custom_call" | custom-call | tf_op jit(solution)/shard_map/finish/pallas_call | solution.py:540
